TPU v7x, 32 devices: a whole 2x2x4 slice. The times are simulated.
32 devices in a mesh: parts: 2 (over y), patch: 4 (over z), sub: 4 (over x, core).
Axes of the slice: x: 2, y: 2, z: 4, core: 2. Of those that a mesh axis runs over, the one named last changes fastest.
Arguments:
- node_latents: bfloat16 [4096, 512], P(('parts', 'patch', 'sub')), parts along dimension 0, may hold values from -6 to 6
- edge_latents: bfloat16 [16384, 512], P(('parts', 'patch', 'sub')), parts along dimension 0, may hold values from -6 to 6
- coarse_edges: bfloat16 [2048, 512], P(('parts', 'patch', 'sub')), parts along dimension 0, may hold values from -6 to 6
- w_edge_in: bfloat16 [1536, 512], replicated, may hold values from -0.15625 to 0.15625
- w_edge_out: bfloat16 [512, 512], replicated, may hold values from -0.25 to 0.25
- w_node_in: bfloat16 [1024, 512], replicated, may hold values from -0.1875 to 0.1875
- w_node_out: bfloat16 [512, 512], replicated, may hold values from -0.25 to 0.25
- fine_senders: int32 [16384], P(('parts', 'patch', 'sub')), parts along dimension 0, may hold values from 0 to 159
- fine_receivers: int32 [16384], P(('parts', 'patch', 'sub')), parts along dimension 0, may hold values from -1 to 127, as said below
- halo_lists: int32 [32, 2, 16], P(('parts', 'patch', 'sub')), parts along dimension 0, may hold values from 0 to 127, as said below
- coarse_senders: int32 [2048], P(('parts', 'patch', 'sub')), parts along dimension 0, may hold values from 0 to 63
- coarse_receivers: int32 [2048], P(('parts', 'patch', 'sub')), parts along dimension 0, may hold values from 0 to 63
Outputs:
- new_nodes: bfloat16 [4096, 512], P(('parts', 'patch', 'sub')), parts along dimension 0
- new_edges: bfloat16 [16384, 512], P(('parts', 'patch', 'sub')), parts along dimension 0
- new_coarse: bfloat16 [2048, 512], P(('parts', 'patch', 'sub')), parts along dimension 0
There are 2 independent parts, one for each index of `parts`. A program takes and returns all parts, laid end to end along the dimension named above; an argument that names none is the same for every part. Nothing has to cross between parts.
Inputs may be any that keep to these rules, and one draw needn't show every extreme that they name: `fine_receivers`: in each device's block of 512 slots the used slots come first and name a local row; the rest hold -1. At least half of a device's slots are used, and some device uses all of them. `halo_lists`: each of a device's two lists holds 16 distinct local rows.
All inputs are finite; a program needn't handle non-finite values.
Results may differ from a plain program's by a relative error of at most 0.0053.
Values may be sent and summed in bfloat16 or wider, within the bound.
A program may use at most 64 MiB of HBM per device.

v0:
```python
import functools

import jax
import jax.numpy as jnp
from jax import lax
from jax.experimental import pallas as pl
from jax.experimental.pallas import tpu as pltpu
from jax.sharding import PartitionSpec as P

CO_DEV = 4
FIRST = 16
F32 = jnp.float32
BF16 = jnp.bfloat16
MESH = pl.DeviceIdType.MESH


def dot(a, b, dims=((1,), (0,))):
    return lax.dot_general(a, b, (dims, ((), ())), preferred_element_type=F32)


def silu(v):
    half = 0.5 * v
    return (half + half * jnp.tanh(half)).astype(BF16)


def norm_rows(values):
    mean = jnp.mean(values, axis=-1, keepdims=True)
    centred = values - mean
    return centred * lax.rsqrt(jnp.mean(centred * centred, axis=-1, keepdims=True) + 1e-05)


def column(row):
    n = row.shape[1]
    wide = jnp.broadcast_to(row.astype(F32), (8, n))
    return jnp.transpose(wide)[:, :1]


def hot(col, first, count):
    lanes = lax.broadcasted_iota(jnp.int32, (col.shape[0], count), 1) + first
    return (col == lanes.astype(F32)).astype(BF16)


def hot_t(row, count):
    rows = lax.broadcasted_iota(jnp.int32, (count, row.shape[1]), 0)
    return (rows == row).astype(BF16)


def each(count, step):
    if count <= 16:
        for i in range(count):
            step(i)
    else:
        def run(i, carry):
            step(i)
            return carry

        lax.fori_loop(0, count, run, 0)


def node_rows(rows, pre, w_out):
    return (rows.astype(F32) + norm_rows(dot(silu(pre), w_out))).astype(BF16)


def kernel(
    n_patch, n_sub,
    nodes_h, edges_h, ced_h, wei_h, weo_h, wni_h, wno_h, fs_h, fr_h, hl_h, cs_h, cr_h,
    n_rows, ne_v, nc_v, nodes_v, n_pre, top, wni_v, wno_v,
    edges_v, ced_v, wei_v, weo_v, fs_v, fr_v, hl_v, cs_v, cr_v,
    head_s, heads_r, heads_f, halo_s, halo_r, part_f, part_s, part_r,
    acc, in_sem, ag_s, ag_r, halo_ss, halo_rs, rs_s, rs_r,
):
    group = n_patch * n_sub
    mp, ms = lax.axis_index("patch"), lax.axis_index("sub")
    me = mp * n_sub + ms
    nodes_n, d = nodes_v.shape
    edges_n = edges_v.shape[0]
    halo = halo_s.shape[1]
    co = heads_r.shape[1]

    def peer_of(k):
        far, side = lax.div(k, n_sub), lax.rem(k, n_sub)
        return (jnp.where(2 * mp < n_patch, n_patch - 1 - far, far),
                jnp.where(2 * ms < n_sub, n_sub - 1 - side, side))

    def rows_of(i):
        start = i * 2 * co
        return pl.ds(start if isinstance(i, int) else pl.multiple_of(start, 2 * co), 2 * co)

    mine = (jnp.where(2 * mp < n_patch, n_patch - 1 - mp, mp) * n_sub
            + jnp.where(2 * ms < n_sub, n_sub - 1 - ms, ms))

    def others(step):
        def run(j):
            k = j + jnp.where(j >= mine, 1, 0)
            step(*peer_of(k))

        each(group - 1, run)

    barrier = pltpu.get_barrier_semaphore()
    others(lambda p, s: pl.semaphore_signal(
        barrier, inc=1, device_id={"patch": p, "sub": s}, device_id_type=MESH))

    pairs = [
        (nodes_h, nodes_v), (hl_h, hl_v), (fs_h, fs_v), (fr_h, fr_v), (cs_h, cs_v), (cr_h, cr_v),
        (wei_h, wei_v), (edges_h, edges_v), (ced_h, ced_v),
        (weo_h, weo_v), (wni_h, wni_v), (wno_h, wno_v),
    ]
    loads = [pltpu.make_async_copy(h, v, in_sem.at[i]) for i, (h, v) in enumerate(pairs)]
    for copy in loads:
        copy.start()
    (l_nodes, l_hl, l_fs, l_fr, l_cs, l_cr, l_wei, l_edges, l_ced, l_weo, l_wni, l_wno) = loads

    l_nodes.wait()
    nodes = nodes_v[...]
    head = nodes[:co]
    head_s[...] = head
    heads_r[me] = head
    pl.semaphore_wait(barrier, group - 1)

    def send_head(p, s):
        pltpu.make_async_remote_copy(
            src_ref=head_s, dst_ref=heads_r.at[me], send_sem=ag_s, recv_sem=ag_r,
            device_id={"patch": p, "sub": s}, device_id_type=MESH).start()

    others(send_head)
    l_hl.wait()
    for side in range(2):
        pick = hot_t(hl_v[0, side:side + 1, :], nodes_n)
        halo_s[side] = dot(pick, nodes, ((0,), (0,))).astype(BF16)

    halos = []
    for side, by in ((0, 1), (1, group - 1)):
        to = lax.rem(me + by, group)
        halos.append(pltpu.make_async_remote_copy(
            src_ref=halo_s.at[side], dst_ref=halo_r.at[side],
            send_sem=halo_ss.at[side], recv_sem=halo_rs.at[side],
            device_id={"patch": to // n_sub, "sub": lax.rem(to, n_sub)}, device_id_type=MESH))
        halos[-1].start()

    l_fs.wait()
    l_fr.wait()
    l_cs.wait()
    l_cr.wait()
    fs, fr = fs_v[...], fr_v[...]
    fs_col = column(jnp.where(fs < halo, fs + (nodes_n + halo), fs - halo))
    fr_col = column(fr)

    l_wei.wait()
    own = jnp.concatenate(
        [dot(nodes, wei_v[d:2 * d]).astype(BF16), dot(nodes, wei_v[2 * d:]).astype(BF16)], axis=0)
    sel = jnp.concatenate([hot(fs_col, 0, nodes_n), hot(fr_col, 0, nodes_n)], axis=1)
    l_edges.wait()
    l_ced.wait()
    acc[...] = dot(edges_v[...], wei_v[:d]) + dot(sel, own)
    ced = ced_v[...]
    ced_pre = dot(ced, wei_v[:d])
    cs, cr = cs_v[...], cr_v[...]
    picks = hot_t(cr, group * co)
    ends = jnp.concatenate([hot(column(cs), 0, group * co), hot(column(cr), 0, group * co)], axis=0)
    l_weo.wait()
    l_wni.wait()
    l_wno.wait()

    many = heads_r.at[pl.ds(0, group - 1)]
    pltpu.make_async_copy(many, many, ag_r).wait()

    def flat(i):
        both = jnp.concatenate([heads_r[2 * i].astype(F32), heads_r[2 * i + 1].astype(F32)], axis=0)
        heads_f[rows_of(i), :] = both

    each(group // 2, flat)
    heads = heads_f[...].astype(BF16)
    c_ends = dot(ends, heads).astype(BF16)
    count = ced.shape[0]
    c_in = jnp.concatenate([c_ends[:count], c_ends[count:]], axis=1)
    c_hid = silu(ced_pre + dot(c_in, wei_v[d:]))
    c_new = (ced.astype(F32) + norm_rows(dot(c_hid, weo_v[...]))).astype(BF16)
    part_f[...] = dot(picks, c_new)

    def pack(i):
        both = part_f[rows_of(i), :].astype(BF16)
        part_s[2 * i] = both[:co]
        part_s[2 * i + 1] = both[co:]

    each(group // 2, pack)

    def send_part(p, s):
        pltpu.make_async_remote_copy(
            src_ref=part_s.at[p * n_sub + s], dst_ref=part_r.at[me], send_sem=rs_s, recv_sem=rs_r,
            device_id={"patch": p, "sub": s}, device_id_type=MESH).start()

    others(send_part)
    part_r[me] = part_s[me]
    nc_v[...] = c_new

    for copy in halos:
        copy.wait_recv()
    far = dot(jnp.concatenate([halo_r[1], halo_r[0]], axis=0), wei_v[d:2 * d]).astype(BF16)
    hid = silu(acc[...] + dot(hot(fs_col, nodes_n, 2 * halo), far))
    delta = norm_rows(dot(hid, weo_v[...]))
    e_new = (edges_v[...].astype(F32) + jnp.where(fr_col >= 0.0, delta, 0.0)).astype(BF16)
    ne_v[...] = e_new
    fine = dot(hot_t(fr, nodes_n), e_new)

    pre = dot(nodes, wni_v[:d])
    n_rows[...] = node_rows(nodes, pre + dot(fine.astype(BF16), wni_v[d:]), wno_v[...])
    first = top.shape[0]
    n_pre[...] = pre[:first]
    top[...] = fine[:first]

    many_p = part_r.at[pl.ds(0, group - 1)]
    pltpu.make_async_copy(many_p, many_p, rs_r).wait()
    top[:co] += jnp.sum(part_r[...].astype(F32), axis=0)

    pltpu.make_async_copy(many, many, ag_s).wait()
    pltpu.make_async_copy(many_p, many_p, rs_s).wait()
    for copy in halos:
        copy.wait_send()


def finish(n_rows, ne_v, nc_v, nodes_v, n_pre, top, wni_v, wno_v, nn_h, ne_h, nc_h, first_v, sem):
    first, d = top.shape
    n = n_rows.shape[0]
    copies = [
        pltpu.make_async_copy(ne_v, ne_h, sem.at[0]),
        pltpu.make_async_copy(nc_v, nc_h, sem.at[1]),
        pltpu.make_async_copy(n_rows.at[pl.ds(first, n - first)], nn_h.at[pl.ds(first, n - first)],
                              sem.at[2]),
    ]
    for copy in copies:
        copy.start()
    pre = n_pre[...] + dot(top[...].astype(BF16), wni_v[d:])
    first_v[...] = node_rows(nodes_v[:first], pre, wno_v[...])
    copies.append(pltpu.make_async_copy(first_v, nn_h.at[pl.ds(0, first)], sem.at[3]))
    copies[-1].start()
    for copy in copies:
        copy.wait()


def body(n_patch, n_sub, *args):
    nodes, edges, ced, wei, weo, wni, wno, fs, fr, hl, cs, cr = args
    fs, fr, cs, cr = (x.reshape(1, -1) for x in (fs, fr, cs, cr))
    operands = (nodes, edges, ced, wei, weo, wni, wno, fs, fr, hl, cs, cr)
    group = n_patch * n_sub
    n, d = nodes.shape
    e, c = edges.shape[0], ced.shape[0]
    halo = hl.shape[2]
    anywhere = pl.BlockSpec(memory_space=pl.ANY)
    inside = pl.BlockSpec(memory_space=pltpu.VMEM)
    dma = pltpu.SemaphoreType.DMA
    kept = [
        pltpu.VMEM((n, d), BF16),
        pltpu.VMEM((e, d), BF16),
        pltpu.VMEM((c, d), BF16),
        pltpu.VMEM((n, d), BF16),
        pltpu.VMEM((FIRST, d), F32),
        pltpu.VMEM((FIRST, d), F32),
        pltpu.VMEM(wni.shape, BF16),
        pltpu.VMEM(wno.shape, BF16),
    ]
    scratch = [pltpu.VMEM(x.shape, x.dtype) for x in (edges, ced, wei, weo, fs, fr, hl, cs, cr)] + [
        pltpu.VMEM((CO_DEV, d), BF16),
        pltpu.VMEM((group, CO_DEV, d), BF16),
        pltpu.VMEM((group * CO_DEV, d), F32),
        pltpu.VMEM((2, halo, d), BF16),
        pltpu.VMEM((2, halo, d), BF16),
        pltpu.VMEM((group * CO_DEV, d), F32),
        pltpu.VMEM((group, CO_DEV, d), BF16),
        pltpu.VMEM((group, CO_DEV, d), BF16),
        pltpu.VMEM((e, d), F32),
        dma((12,)), dma, dma, dma((2,)), dma((2,)), dma, dma,
    ]
    held = pl.pallas_call(
        functools.partial(kernel, n_patch, n_sub),
        out_shape=kept,
        in_specs=[anywhere] * len(operands),
        out_specs=[inside] * len(kept),
        scratch_shapes=scratch,
        compiler_params=pltpu.CompilerParams(
            collective_id=0, has_side_effects=True, vmem_limit_bytes=60 * 1024 * 1024),
        name="layer",
    )(*operands)
    return pl.pallas_call(
        finish,
        out_shape=[jax.ShapeDtypeStruct(x.shape, BF16) for x in (nodes, edges, ced)],
        in_specs=[inside] * len(kept),
        out_specs=[anywhere] * 3,
        scratch_shapes=[pltpu.VMEM((FIRST, d), BF16), dma((4,))],
        compiler_params=pltpu.CompilerParams(vmem_limit_bytes=8 * 1024 * 1024),
        name="finish",
    )(*held)


def solution(mesh):
    rows = P(("parts", "patch", "sub"), None)
    ids = P(("parts", "patch", "sub"))
    in_specs = (rows, rows, rows, P(), P(), P(), P(), ids, ids,
                P(("parts", "patch", "sub"), None, None), ids, ids)
    run = functools.partial(body, mesh.shape["patch"], mesh.shape["sub"])
    return jax.shard_map(run, mesh=mesh, in_specs=in_specs, out_specs=(rows, rows, rows),
                         check_vma=False)
```

profile of v0, /device:TPU:0, one launch (start us, length us, event | category | flops | bytes accessed | tf_op | source)
XLA Modules:
  0.0 17.0 jit_solution(758998629049357554)
XLA Ops:
  0.6 15.2 %layer.1 = (bf16[128,512]{1,0:T(8,128)(2,1)S(1)}, bf16[512,512]{1,0:T(8,128)(2,1)S(1)}, bf16[64,512]{1,0:T(8,128)(2,1)S(1)}, bf16[128,512]{1,0:T(8,128)(2,1)S(1)...) custom-call(bf16[128,512]{1,0:T(8,128)(2,1)} %nodes_h.1, ...), custom_call_target="tpu_custom_call" | custom-call | tf_op jit(solution)/shard_map/layer/pallas_call | solution.py:273
  15.8 1.2 %finish.1 = (bf16[128,512]{1,0:T(8,128)(2,1)}, bf16[512,512]{1,0:T(8,128)(2,1)}, bf16[64,512]{1,0:T(8,128)(2,1)}) custom-call(bf16[128,512]{1,0:T(8,128)(2,1)S(1)} %get-tuple-element.11.n_rows, bf16[512,512]{1,0:T(8,128)(2,1)S(1)} %get-tuple-element.12.ne_v, bf16[64,512]{1,0:T(8,128)(2,1)S(1)} %get-tuple-element.13.nc_v, ...), custom_call_target="tpu_custom_call" | custom-call | tf_op jit(solution)/shard_map/finish/pallas_call | solution.py:283
where the time goes:
time: 17.1 us; the launch traced here: 17 us
  Pallas kernels  16.3 us (95%)
  between operations  0.64 us (4%)
    pallas_call x1, Pallas kernels, body(): pl.pallas_call(functools.partial(kernel, n_patch, n_sub), out_shape=kept,...  15.2 us
    pallas_call x1, Pallas kernels, body(): pl.pallas_call(finish, out_shape=[jax.ShapeDtypeStruct(x.shape, BF16) for...  1.16 us

commit v1 on v0

--- a/solution.py
+++ b/solution.py
@@ -66,39 +66,87 @@
     nodes_h, edges_h, ced_h, wei_h, weo_h, wni_h, wno_h, fs_h, fr_h, hl_h, cs_h, cr_h,
     n_rows, ne_v, nc_v, nodes_v, n_pre, top, wni_v, wno_v,
     edges_v, ced_v, wei_v, weo_v, fs_v, fr_v, hl_v, cs_v, cr_v,
-    head_s, heads_r, heads_f, halo_s, halo_r, part_f, part_s, part_r,
-    acc, in_sem, ag_s, ag_r, halo_ss, halo_rs, rs_s, rs_r,
+    mate_v, mate_new, mate_cs, mate_cr,
+    heads_r, heads_f, halo_s, halo_r, part_f, part_s, part_r,
+    acc, in_sem, ag_s, ag_r, halo_ss, halo_rs, rs_s, rs_r, mate_s, mate_r, back_s, back_r, near, go,
 ):
-    group = n_patch * n_sub
+    half_p = n_patch // 2
+    group, half = n_patch * n_sub, half_p * n_sub
     mp, ms = lax.axis_index("patch"), lax.axis_index("sub")
     me = mp * n_sub + ms
+    hub = mp < half_p
+    leaf = mp >= half_p
     nodes_n, d = nodes_v.shape
     edges_n = edges_v.shape[0]
     halo = halo_s.shape[1]
     co = heads_r.shape[1]
-
-    def peer_of(k):
-        far, side = lax.div(k, n_sub), lax.rem(k, n_sub)
-        return (jnp.where(2 * mp < n_patch, n_patch - 1 - far, far),
-                jnp.where(2 * ms < n_sub, n_sub - 1 - side, side))
+    count = ced_v.shape[0]
 
     def rows_of(i):
         start = i * 2 * co
         return pl.ds(start if isinstance(i, int) else pl.multiple_of(start, 2 * co), 2 * co)
 
-    mine = (jnp.where(2 * mp < n_patch, n_patch - 1 - mp, mp) * n_sub
-            + jnp.where(2 * ms < n_sub, n_sub - 1 - ms, ms))
-
-    def others(step):
-        def run(j):
-            k = j + jnp.where(j >= mine, 1, 0)
-            step(*peer_of(k))
-
-        each(group - 1, run)
+    def turn(i, by, n):
+        at = i + by
+        return jnp.where(at >= n, at - n, at)
+
+    def device(p, s):
+        return {"device_id": {"patch": p, "sub": s}, "device_id_type": MESH}
+
+    def device_of(i):
+        return device(lax.div(i, n_sub), lax.rem(i, n_sub))
+
+    def patch(p, step, own=True):
+        for j in range(1, n_sub):
+            step(p, turn(ms, j, n_sub))
+        if own:
+            step(p, ms)
+
+    def other_hubs(step):
+        each(half_p - 1, lambda i: patch(turn(mp, i + 1, half_p), step))
+        patch(mp, step, own=False)
+
+    def leaves(step):
+        each(half_p, lambda i: patch(n_patch - 1 - i, step))
 
     barrier = pltpu.get_barrier_semaphore()
-    others(lambda p, s: pl.semaphore_signal(
-        barrier, inc=1, device_id={"patch": p, "sub": s}, device_id_type=MESH))
+
+    @pl.when(hub)
+    def _():
+        def hail(p, s):
+            pl.semaphore_signal(barrier, inc=1, **device(p, s))
+
+        other_hubs(hail)
+        leaves(hail)
+
+    row = nodes_h.at[pl.ds(0, co)]
+
+    def send_head(p, s):
+        pltpu.make_async_remote_copy(
+            src_ref=row, dst_ref=heads_r.at[me], send_sem=ag_s, recv_sem=ag_r,
+            **device(p, s)).start()
+
+    to_hub = device(mp - half_p, ms)
+    visit = [
+        pltpu.make_async_remote_copy(
+            src_ref=src, dst_ref=dst, send_sem=mate_s.at[i], recv_sem=mate_r.at[i], **to_hub)
+        for i, (src, dst) in enumerate(((cs_h, mate_cs), (cr_h, mate_cr), (ced_h, mate_v)))
+    ]
+    back = pltpu.make_async_remote_copy(
+        src_ref=mate_new, dst_ref=mate_v, send_sem=back_s, recv_sem=back_r,
+        **device(mp + half_p, ms))
+
+    @pl.when(leaf)
+    def _():
+        pl.semaphore_wait(barrier, half)
+        for copy in visit:
+            copy.start()
+        each(half_p, lambda p: patch(p, send_head))
+        pl.semaphore_signal(near, inc=1, **to_hub)
+        for by in (1, group - 1):
+            beside = turn(me, by, group)
+            pl.semaphore_signal(
+                near, inc=1, **device_of(jnp.where(beside < half, beside, beside - half)))
 
     pairs = [
         (nodes_h, nodes_v), (hl_h, hl_v), (fs_h, fs_v), (fr_h, fr_v), (cs_h, cs_v), (cr_h, cr_v),
@@ -112,30 +160,25 @@
 
     l_nodes.wait()
     nodes = nodes_v[...]
-    head = nodes[:co]
-    head_s[...] = head
-    heads_r[me] = head
-    pl.semaphore_wait(barrier, group - 1)
-
-    def send_head(p, s):
-        pltpu.make_async_remote_copy(
-            src_ref=head_s, dst_ref=heads_r.at[me], send_sem=ag_s, recv_sem=ag_r,
-            device_id={"patch": p, "sub": s}, device_id_type=MESH).start()
-
-    others(send_head)
     l_hl.wait()
     for side in range(2):
         pick = hot_t(hl_v[0, side:side + 1, :], nodes_n)
         halo_s[side] = dot(pick, nodes, ((0,), (0,))).astype(BF16)
 
-    halos = []
+    @pl.when(hub)
+    def _():
+        heads_r[me] = nodes_v[:co]
+        pl.semaphore_wait(barrier, half - 1)
+        other_hubs(send_head)
+
+    halos, soon = [], []
     for side, by in ((0, 1), (1, group - 1)):
-        to = lax.rem(me + by, group)
+        to = turn(me, by, group)
+        soon.append(to < half)
         halos.append(pltpu.make_async_remote_copy(
             src_ref=halo_s.at[side], dst_ref=halo_r.at[side],
-            send_sem=halo_ss.at[side], recv_sem=halo_rs.at[side],
-            device_id={"patch": to // n_sub, "sub": lax.rem(to, n_sub)}, device_id_type=MESH))
-        halos[-1].start()
+            send_sem=halo_ss.at[side], recv_sem=halo_rs.at[side], **device_of(to)))
+        pl.when(soon[-1])(halos[-1].start)
 
     l_fs.wait()
     l_fr.wait()
@@ -152,46 +195,72 @@
     l_edges.wait()
     l_ced.wait()
     acc[...] = dot(edges_v[...], wei_v[:d]) + dot(sel, own)
-    ced = ced_v[...]
-    ced_pre = dot(ced, wei_v[:d])
-    cs, cr = cs_v[...], cr_v[...]
-    picks = hot_t(cr, group * co)
-    ends = jnp.concatenate([hot(column(cs), 0, group * co), hot(column(cr), 0, group * co)], axis=0)
     l_weo.wait()
     l_wni.wait()
     l_wno.wait()
 
-    many = heads_r.at[pl.ds(0, group - 1)]
-    pltpu.make_async_copy(many, many, ag_r).wait()
-
-    def flat(i):
-        both = jnp.concatenate([heads_r[2 * i].astype(F32), heads_r[2 * i + 1].astype(F32)], axis=0)
-        heads_f[rows_of(i), :] = both
-
-    each(group // 2, flat)
-    heads = heads_f[...].astype(BF16)
-    c_ends = dot(ends, heads).astype(BF16)
-    count = ced.shape[0]
-    c_in = jnp.concatenate([c_ends[:count], c_ends[count:]], axis=1)
-    c_hid = silu(ced_pre + dot(c_in, wei_v[d:]))
-    c_new = (ced.astype(F32) + norm_rows(dot(c_hid, weo_v[...]))).astype(BF16)
-    part_f[...] = dot(picks, c_new)
-
-    def pack(i):
-        both = part_f[rows_of(i), :].astype(BF16)
-        part_s[2 * i] = both[:co]
-        part_s[2 * i + 1] = both[co:]
-
-    each(group // 2, pack)
-
-    def send_part(p, s):
-        pltpu.make_async_remote_copy(
-            src_ref=part_s.at[p * n_sub + s], dst_ref=part_r.at[me], send_sem=rs_s, recv_sem=rs_r,
-            device_id={"patch": p, "sub": s}, device_id_type=MESH).start()
-
-    others(send_part)
-    part_r[me] = part_s[me]
-    nc_v[...] = c_new
+    @pl.when(hub)
+    def _():
+        pl.semaphore_wait(near, 3)
+        pl.semaphore_signal(go, inc=1, **device(mp + half_p, ms))
+
+    @pl.when(leaf)
+    def _():
+        pl.semaphore_wait(go, 1)
+
+    for early, copy in zip(soon, halos):
+        pl.when(jnp.logical_not(early))(copy.start)
+
+    @pl.when(hub)
+    def _():
+        ced = ced_v[...]
+        ced_pre = dot(ced, wei_v[:d])
+        visit[0].wait_recv()
+        visit[1].wait_recv()
+        cs = jnp.concatenate([cs_v[...], mate_cs[...]], axis=1)
+        cr = jnp.concatenate([cr_v[...], mate_cr[...]], axis=1)
+        picks = hot_t(cr, group * co)
+        ends = jnp.concatenate(
+            [hot(column(cs), 0, group * co), hot(column(cr), 0, group * co)], axis=0)
+
+        many = heads_r.at[pl.ds(0, group - 1)]
+        pltpu.make_async_copy(many, many, ag_r).wait()
+
+        def flat(i):
+            both = jnp.concatenate(
+                [heads_r[2 * i].astype(F32), heads_r[2 * i + 1].astype(F32)], axis=0)
+            heads_f[rows_of(i), :] = both
+
+        each(group // 2, flat)
+        heads = heads_f[...].astype(BF16)
+        c_ends = dot(ends, heads).astype(BF16)
+        c_in = jnp.concatenate([c_ends[:2 * count], c_ends[2 * count:]], axis=1)
+        c_pre = dot(c_in, wei_v[d:])
+        visit[2].wait_recv()
+        mate = mate_v[...]
+        both = jnp.concatenate([ced, mate], axis=0)
+        c_hid = silu(c_pre + jnp.concatenate([ced_pre, dot(mate, wei_v[:d])], axis=0))
+        c_new = (both.astype(F32) + norm_rows(dot(c_hid, weo_v[...]))).astype(BF16)
+        part_f[...] = dot(picks, c_new)
+
+        def pack(i):
+            both = part_f[rows_of(i), :].astype(BF16)
+            part_s[2 * i] = both[:co]
+            part_s[2 * i + 1] = both[co:]
+
+        each(group // 2, pack)
+
+        def send_part(p, s):
+            pltpu.make_async_remote_copy(
+                src_ref=part_s.at[p * n_sub + s], dst_ref=part_r.at[me],
+                send_sem=rs_s, recv_sem=rs_r, **device(p, s)).start()
+
+        other_hubs(send_part)
+        leaves(send_part)
+        mate_new[...] = c_new[count:]
+        back.start()
+        part_r[me] = part_s[me]
+        nc_v[...] = c_new[:count]
 
     for copy in halos:
         copy.wait_recv()
@@ -208,14 +277,30 @@
     n_pre[...] = pre[:first]
     top[...] = fine[:first]
 
-    many_p = part_r.at[pl.ds(0, group - 1)]
-    pltpu.make_async_copy(many_p, many_p, rs_r).wait()
-    top[:co] += jnp.sum(part_r[...].astype(F32), axis=0)
-
-    pltpu.make_async_copy(many, many, ag_s).wait()
-    pltpu.make_async_copy(many_p, many_p, rs_s).wait()
     for copy in halos:
         copy.wait_send()
+
+    def await_rows(number, sem):
+        span = heads_r.at[pl.ds(0, number)]
+        pltpu.make_async_copy(span, span, sem).wait()
+
+    @pl.when(hub)
+    def _():
+        await_rows(half - 1, ag_s)
+        await_rows(group - 1, rs_s)
+        back.wait_send()
+        await_rows(half - 1, rs_r)
+
+    @pl.when(leaf)
+    def _():
+        await_rows(half, ag_s)
+        for copy in visit:
+            copy.wait_send()
+        back.wait_recv()
+        nc_v[...] = mate_v[...]
+        await_rows(half, rs_r)
+
+    top[:co] += jnp.sum(part_r[...].astype(F32), axis=0)
 
 
 def finish(n_rows, ne_v, nc_v, nodes_v, n_pre, top, wni_v, wno_v, nn_h, ne_h, nc_h, first_v, sem):
@@ -259,16 +344,20 @@
         pltpu.VMEM(wno.shape, BF16),
     ]
     scratch = [pltpu.VMEM(x.shape, x.dtype) for x in (edges, ced, wei, weo, fs, fr, hl, cs, cr)] + [
-        pltpu.VMEM((CO_DEV, d), BF16),
+        pltpu.VMEM((c, d), BF16),
+        pltpu.VMEM((c, d), BF16),
+        pltpu.VMEM(cs.shape, cs.dtype),
+        pltpu.VMEM(cr.shape, cr.dtype),
         pltpu.VMEM((group, CO_DEV, d), BF16),
         pltpu.VMEM((group * CO_DEV, d), F32),
         pltpu.VMEM((2, halo, d), BF16),
         pltpu.VMEM((2, halo, d), BF16),
         pltpu.VMEM((group * CO_DEV, d), F32),
         pltpu.VMEM((group, CO_DEV, d), BF16),
-        pltpu.VMEM((group, CO_DEV, d), BF16),
+        pltpu.VMEM((group // 2, CO_DEV, d), BF16),
         pltpu.VMEM((e, d), F32),
-        dma((12,)), dma, dma, dma((2,)), dma((2,)), dma, dma,
+        dma((12,)), dma, dma, dma((2,)), dma((2,)), dma, dma, dma((3,)), dma((3,)), dma, dma,
+        pltpu.SemaphoreType.REGULAR, pltpu.SemaphoreType.REGULAR,
     ]
     held = pl.pallas_call(
         functools.partial(kernel, n_patch, n_sub),

time: 17.1 us -> 17.7 us (1.035)
  the two profiles are of different devices: /device:TPU:0 before, /device:TPU:21 now
where the time goes in v1:
time: 17.7 us; the launch traced here: 17.5 us
  Pallas kernels  16.9 us (95%)
  between operations  0.64 us (4%)
    pallas_call x1, Pallas kernels, body(): pl.pallas_call(functools.partial(kernel, n_patch, n_sub), out_shape=kept,...  15.7 us
    pallas_call x1, Pallas kernels, body(): pl.pallas_call(finish, out_shape=[jax.ShapeDtypeStruct(x.shape, BF16) for...  1.16 us

profile of v1, /device:TPU:21, one launch (start us, length us, event | category | flops | bytes accessed | tf_op | source)
XLA Modules:
  0.0 17.5 jit_solution(4984235383130000220)
XLA Ops:
  0.6 15.7 %layer.1 = (bf16[128,512]{1,0:T(8,128)(2,1)S(1)}, bf16[512,512]{1,0:T(8,128)(2,1)S(1)}, bf16[64,512]{1,0:T(8,128)(2,1)S(1)}, bf16[128,512]{1,0:T(8,128)(2,1)S(1)...) custom-call(bf16[128,512]{1,0:T(8,128)(2,1)} %nodes_h.1, ...), custom_call_target="tpu_custom_call" | custom-call | tf_op jit(solution)/shard_map/layer/pallas_call | solution.py:362
  16.4 1.2 %finish.1 = (bf16[128,512]{1,0:T(8,128)(2,1)}, bf16[512,512]{1,0:T(8,128)(2,1)}, bf16[64,512]{1,0:T(8,128)(2,1)}) custom-call(bf16[128,512]{1,0:T(8,128)(2,1)S(1)} %get-tuple-element.11.n_rows, bf16[512,512]{1,0:T(8,128)(2,1)S(1)} %get-tuple-element.12.ne_v, bf16[64,512]{1,0:T(8,128)(2,1)S(1)} %get-tuple-element.13.nc_v, ...), custom_call_target="tpu_custom_call" | custom-call | tf_op jit(solution)/shard_map/finish/pallas_call | solution.py:372

commit v2 on v1

--- a/solution.py
+++ b/solution.py
@@ -70,12 +70,12 @@
     heads_r, heads_f, halo_s, halo_r, part_f, part_s, part_r,
     acc, in_sem, ag_s, ag_r, halo_ss, halo_rs, rs_s, rs_r, mate_s, mate_r, back_s, back_r, near, go,
 ):
-    half_p = n_patch // 2
-    group, half = n_patch * n_sub, half_p * n_sub
+    group, shift = n_patch * n_sub, n_sub
+    hubs = group - shift
     mp, ms = lax.axis_index("patch"), lax.axis_index("sub")
     me = mp * n_sub + ms
-    hub = mp < half_p
-    leaf = mp >= half_p
+    hub, leaf = me < hubs, me >= hubs
+    hosts = (me >= hubs - shift) & hub
     nodes_n, d = nodes_v.shape
     edges_n = edges_v.shape[0]
     halo = halo_s.shape[1]
@@ -90,63 +90,58 @@
         at = i + by
         return jnp.where(at >= n, at - n, at)
 
-    def device(p, s):
-        return {"device_id": {"patch": p, "sub": s}, "device_id_type": MESH}
-
-    def device_of(i):
-        return device(lax.div(i, n_sub), lax.rem(i, n_sub))
-
-    def patch(p, step, own=True):
-        for j in range(1, n_sub):
-            step(p, turn(ms, j, n_sub))
-        if own:
-            step(p, ms)
-
-    def other_hubs(step):
-        each(half_p - 1, lambda i: patch(turn(mp, i + 1, half_p), step))
-        patch(mp, step, own=False)
-
-    def leaves(step):
-        each(half_p, lambda i: patch(n_patch - 1 - i, step))
+    def device(i):
+        if isinstance(i, int):
+            at = {"patch": i // n_sub, "sub": i % n_sub}
+        else:
+            at = {"patch": lax.div(i, n_sub), "sub": lax.rem(i, n_sub)}
+        return {"device_id": at, "device_id_type": MESH}
+
+    def others(count, step):
+        each(count, lambda i: pl.when(i != me)(lambda: step(i)))
+
+    def await_rows(number, sem):
+        span = heads_r.at[pl.ds(0, number)]
+        pltpu.make_async_copy(span, span, sem).wait()
 
     barrier = pltpu.get_barrier_semaphore()
 
     @pl.when(hub)
     def _():
-        def hail(p, s):
-            pl.semaphore_signal(barrier, inc=1, **device(p, s))
-
-        other_hubs(hail)
-        leaves(hail)
+        others(group, lambda i: pl.semaphore_signal(barrier, inc=1, **device(i)))
 
     row = nodes_h.at[pl.ds(0, co)]
 
-    def send_head(p, s):
+    def send_head(i):
         pltpu.make_async_remote_copy(
             src_ref=row, dst_ref=heads_r.at[me], send_sem=ag_s, recv_sem=ag_r,
-            **device(p, s)).start()
-
-    to_hub = device(mp - half_p, ms)
+            **device(i)).start()
+
     visit = [
         pltpu.make_async_remote_copy(
-            src_ref=src, dst_ref=dst, send_sem=mate_s.at[i], recv_sem=mate_r.at[i], **to_hub)
+            src_ref=src, dst_ref=dst, send_sem=mate_s.at[i], recv_sem=mate_r.at[i],
+            **device(me - shift))
         for i, (src, dst) in enumerate(((cs_h, mate_cs), (cr_h, mate_cr), (ced_h, mate_v)))
     ]
     back = pltpu.make_async_remote_copy(
-        src_ref=mate_new, dst_ref=mate_v, send_sem=back_s, recv_sem=back_r,
-        **device(mp + half_p, ms))
+        src_ref=mate_new, dst_ref=mate_v, send_sem=back_s, recv_sem=back_r, **device(me + shift))
+
+    def away(i):
+        return jnp.where(i >= hubs, 1, 0)
+
+    prev, after = turn(me, group - 1, group), turn(me, 1, group)
+    callers = away(prev) + away(after) + jnp.where(
+        hosts, 1 + away(me + shift - 1) + away(turn(me + shift, 1, group)), 0)
 
     @pl.when(leaf)
     def _():
-        pl.semaphore_wait(barrier, half)
+        pl.semaphore_wait(barrier, hubs)
+        each(hubs, lambda i: send_head(hubs - 1 - i))
         for copy in visit:
             copy.start()
-        each(half_p, lambda p: patch(p, send_head))
-        pl.semaphore_signal(near, inc=1, **to_hub)
-        for by in (1, group - 1):
-            beside = turn(me, by, group)
-            pl.semaphore_signal(
-                near, inc=1, **device_of(jnp.where(beside < half, beside, beside - half)))
+        pl.semaphore_signal(near, inc=1, **device(me - shift))
+        for beside in (prev, after):
+            pl.semaphore_signal(near, inc=1, **device(beside - shift * away(beside)))
 
     pairs = [
         (nodes_h, nodes_v), (hl_h, hl_v), (fs_h, fs_v), (fr_h, fr_v), (cs_h, cs_v), (cr_h, cr_v),
@@ -168,16 +163,15 @@
     @pl.when(hub)
     def _():
         heads_r[me] = nodes_v[:co]
-        pl.semaphore_wait(barrier, half - 1)
-        other_hubs(send_head)
+        pl.semaphore_wait(barrier, hubs - 1)
+        each(hubs, lambda i: pl.when(hubs - 1 - i != me)(lambda: send_head(hubs - 1 - i)))
 
     halos, soon = [], []
-    for side, by in ((0, 1), (1, group - 1)):
-        to = turn(me, by, group)
-        soon.append(to < half)
+    for side, to in ((0, after), (1, prev)):
+        soon.append(to < hubs)
         halos.append(pltpu.make_async_remote_copy(
             src_ref=halo_s.at[side], dst_ref=halo_r.at[side],
-            send_sem=halo_ss.at[side], recv_sem=halo_rs.at[side], **device_of(to)))
+            send_sem=halo_ss.at[side], recv_sem=halo_rs.at[side], **device(to)))
         pl.when(soon[-1])(halos[-1].start)
 
     l_fs.wait()
@@ -199,32 +193,30 @@
     l_wni.wait()
     l_wno.wait()
 
-    @pl.when(hub)
-    def _():
-        pl.semaphore_wait(near, 3)
-        pl.semaphore_signal(go, inc=1, **device(mp + half_p, ms))
-
-    @pl.when(leaf)
-    def _():
-        pl.semaphore_wait(go, 1)
-
+    pl.when(hub & (callers > 0))(lambda: pl.semaphore_wait(near, callers))
+    pl.when(hosts)(lambda: pl.semaphore_signal(go, inc=1, **device(me + shift)))
+    pl.when(leaf)(lambda: pl.semaphore_wait(go, 1))
     for early, copy in zip(soon, halos):
         pl.when(jnp.logical_not(early))(copy.start)
 
-    @pl.when(hub)
-    def _():
-        ced = ced_v[...]
+    def coarse(hosting):
+        ced, cs, cr = ced_v[...], cs_v[...], cr_v[...]
         ced_pre = dot(ced, wei_v[:d])
-        visit[0].wait_recv()
-        visit[1].wait_recv()
-        cs = jnp.concatenate([cs_v[...], mate_cs[...]], axis=1)
-        cr = jnp.concatenate([cr_v[...], mate_cr[...]], axis=1)
+        if hosting:
+            visit[0].wait_recv()
+            visit[1].wait_recv()
+            cs = jnp.concatenate([cs, mate_cs[...]], axis=1)
+            cr = jnp.concatenate([cr, mate_cr[...]], axis=1)
+        rows = cs.shape[1]
         picks = hot_t(cr, group * co)
         ends = jnp.concatenate(
             [hot(column(cs), 0, group * co), hot(column(cr), 0, group * co)], axis=0)
-
-        many = heads_r.at[pl.ds(0, group - 1)]
-        pltpu.make_async_copy(many, many, ag_r).wait()
+        if hosting:
+            visit[2].wait_recv()
+            ced_pre = jnp.concatenate([ced_pre, dot(mate_v[...], wei_v[:d])], axis=0)
+            ced = jnp.concatenate([ced, mate_v[...]], axis=0)
+
+        await_rows(group - 1, ag_r)
 
         def flat(i):
             both = jnp.concatenate(
@@ -234,33 +226,32 @@
         each(group // 2, flat)
         heads = heads_f[...].astype(BF16)
         c_ends = dot(ends, heads).astype(BF16)
-        c_in = jnp.concatenate([c_ends[:2 * count], c_ends[2 * count:]], axis=1)
-        c_pre = dot(c_in, wei_v[d:])
-        visit[2].wait_recv()
-        mate = mate_v[...]
-        both = jnp.concatenate([ced, mate], axis=0)
-        c_hid = silu(c_pre + jnp.concatenate([ced_pre, dot(mate, wei_v[:d])], axis=0))
-        c_new = (both.astype(F32) + norm_rows(dot(c_hid, weo_v[...]))).astype(BF16)
+        c_in = jnp.concatenate([c_ends[:rows], c_ends[rows:]], axis=1)
+        c_hid = silu(ced_pre + dot(c_in, wei_v[d:]))
+        c_new = (ced.astype(F32) + norm_rows(dot(c_hid, weo_v[...]))).astype(BF16)
         part_f[...] = dot(picks, c_new)
+
+        def send_part(i):
+            pltpu.make_async_remote_copy(
+                src_ref=part_s.at[i], dst_ref=part_r.at[me],
+                send_sem=rs_s, recv_sem=rs_r, **device(i)).start()
 
         def pack(i):
             both = part_f[rows_of(i), :].astype(BF16)
-            part_s[2 * i] = both[:co]
-            part_s[2 * i + 1] = both[co:]
+            for j in range(2):
+                at = 2 * i + j
+                part_s[at] = both[j * co:(j + 1) * co]
+                pl.when(me != at)(lambda: send_part(at))
 
         each(group // 2, pack)
-
-        def send_part(p, s):
-            pltpu.make_async_remote_copy(
-                src_ref=part_s.at[p * n_sub + s], dst_ref=part_r.at[me],
-                send_sem=rs_s, recv_sem=rs_r, **device(p, s)).start()
-
-        other_hubs(send_part)
-        leaves(send_part)
-        mate_new[...] = c_new[count:]
-        back.start()
+        if hosting:
+            mate_new[...] = c_new[count:]
+            back.start()
         part_r[me] = part_s[me]
         nc_v[...] = c_new[:count]
+
+    pl.when(hub & jnp.logical_not(hosts))(lambda: coarse(False))
+    pl.when(hosts)(lambda: coarse(True))
 
     for copy in halos:
         copy.wait_recv()
@@ -280,25 +271,22 @@
     for copy in halos:
         copy.wait_send()
 
-    def await_rows(number, sem):
-        span = heads_r.at[pl.ds(0, number)]
-        pltpu.make_async_copy(span, span, sem).wait()
+    pl.when(hosts)(back.wait_send)
 
     @pl.when(hub)
     def _():
-        await_rows(half - 1, ag_s)
+        await_rows(hubs - 1, ag_s)
         await_rows(group - 1, rs_s)
-        back.wait_send()
-        await_rows(half - 1, rs_r)
+        await_rows(hubs - 1, rs_r)
 
     @pl.when(leaf)
     def _():
-        await_rows(half, ag_s)
+        await_rows(hubs, ag_s)
         for copy in visit:
             copy.wait_send()
         back.wait_recv()
         nc_v[...] = mate_v[...]
-        await_rows(half, rs_r)
+        await_rows(hubs, rs_r)
 
     top[:co] += jnp.sum(part_r[...].astype(F32), axis=0)
 
@@ -354,7 +342,7 @@
         pltpu.VMEM((2, halo, d), BF16),
         pltpu.VMEM((group * CO_DEV, d), F32),
         pltpu.VMEM((group, CO_DEV, d), BF16),
-        pltpu.VMEM((group // 2, CO_DEV, d), BF16),
+        pltpu.VMEM((group - n_sub, CO_DEV, d), BF16),
         pltpu.VMEM((e, d), F32),
         dma((12,)), dma, dma, dma((2,)), dma((2,)), dma, dma, dma((3,)), dma((3,)), dma, dma,
         pltpu.SemaphoreType.REGULAR, pltpu.SemaphoreType.REGULAR,

time: 17.7 us -> 15.9 us (0.90)
  the two profiles are of different devices: /device:TPU:21 before, /device:TPU:0 now
where the time goes in v2:
time: 15.9 us; the launch traced here: 15.8 us
  Pallas kernels  15.1 us (95%)
  between operations  0.64 us (4%)
    pallas_call x1, Pallas kernels, body(): pl.pallas_call(functools.partial(kernel, n_patch, n_sub), out_shape=kept,...  14 us
    pallas_call x1, Pallas kernels, body(): pl.pallas_call(finish, out_shape=[jax.ShapeDtypeStruct(x.shape, BF16) for...  1.16 us

profile of v2, /device:TPU:0, one launch (start us, length us, event | category | flops | bytes accessed | tf_op | source)
XLA Modules:
  0.0 15.8 jit_solution(2537961702125621857)
XLA Ops:
  0.6 14.0 %layer.1 = (bf16[128,512]{1,0:T(8,128)(2,1)S(1)}, bf16[512,512]{1,0:T(8,128)(2,1)S(1)}, bf16[64,512]{1,0:T(8,128)(2,1)S(1)}, bf16[128,512]{1,0:T(8,128)(2,1)S(1)...) custom-call(bf16[128,512]{1,0:T(8,128)(2,1)} %nodes_h.1, ...), custom_call_target="tpu_custom_call" | custom-call | tf_op jit(solution)/shard_map/layer/pallas_call | solution.py:350
  14.6 1.2 %finish.1 = (bf16[128,512]{1,0:T(8,128)(2,1)}, bf16[512,512]{1,0:T(8,128)(2,1)}, bf16[64,512]{1,0:T(8,128)(2,1)}) custom-call(bf16[128,512]{1,0:T(8,128)(2,1)S(1)} %get-tuple-element.11.n_rows, bf16[512,512]{1,0:T(8,128)(2,1)S(1)} %get-tuple-element.12.ne_v, bf16[64,512]{1,0:T(8,128)(2,1)S(1)} %get-tuple-element.13.nc_v, ...), custom_call_target="tpu_custom_call" | custom-call | tf_op jit(solution)/shard_map/finish/pallas_call | solution.py:360

commit v3 on v2

--- a/solution.py
+++ b/solution.py
@@ -66,18 +66,17 @@
     nodes_h, edges_h, ced_h, wei_h, weo_h, wni_h, wno_h, fs_h, fr_h, hl_h, cs_h, cr_h,
     n_rows, ne_v, nc_v, nodes_v, n_pre, top, wni_v, wno_v,
     edges_v, ced_v, wei_v, weo_v, fs_v, fr_v, hl_v, cs_v, cr_v,
-    mate_v, mate_new, mate_cs, mate_cr,
+    mate_v, mate_new, mate_ids,
     heads_r, heads_f, halo_s, halo_r, part_f, part_s, part_r,
-    acc, in_sem, ag_s, ag_r, halo_ss, halo_rs, rs_s, rs_r, mate_s, mate_r, back_s, back_r, near, go,
+    acc, in_sem, sent, ag_s, ag_r, halo_rs, rs_s, rs_r, ids_r, mate_r, near,
 ):
     group, shift = n_patch * n_sub, n_sub
+    hub_p = n_patch - 1
     hubs = group - shift
     mp, ms = lax.axis_index("patch"), lax.axis_index("sub")
     me = mp * n_sub + ms
-    hub, leaf = me < hubs, me >= hubs
-    hosts = (me >= hubs - shift) & hub
+    hub, leaf, hosts = mp < hub_p, mp == hub_p, mp == hub_p - 1
     nodes_n, d = nodes_v.shape
-    edges_n = edges_v.shape[0]
     halo = halo_s.shape[1]
     co = heads_r.shape[1]
     count = ced_v.shape[0]
@@ -90,15 +89,23 @@
         at = i + by
         return jnp.where(at >= n, at - n, at)
 
-    def device(i):
+    def device(p, s):
+        return {"device_id": {"patch": p, "sub": s}, "device_id_type": MESH}
+
+    def device_of(i):
         if isinstance(i, int):
-            at = {"patch": i // n_sub, "sub": i % n_sub}
-        else:
-            at = {"patch": lax.div(i, n_sub), "sub": lax.rem(i, n_sub)}
-        return {"device_id": at, "device_id_type": MESH}
-
-    def others(count, step):
-        each(count, lambda i: pl.when(i != me)(lambda: step(i)))
+            return device(i // n_sub, i % n_sub)
+        return device(lax.div(i, n_sub), lax.rem(i, n_sub))
+
+    subs = [ms] + [turn(ms, j, n_sub) for j in range(1, n_sub)]
+
+    def patch(p, step):
+        for s in subs:
+            step(p, s)
+
+    def beside(step):
+        for s in subs[1:]:
+            step(mp, s)
 
     def await_rows(number, sem):
         span = heads_r.at[pl.ds(0, number)]
@@ -106,96 +113,106 @@
 
     barrier = pltpu.get_barrier_semaphore()
 
-    @pl.when(hub)
-    def _():
-        others(group, lambda i: pl.semaphore_signal(barrier, inc=1, **device(i)))
-
-    row = nodes_h.at[pl.ds(0, co)]
-
-    def send_head(i):
-        pltpu.make_async_remote_copy(
-            src_ref=row, dst_ref=heads_r.at[me], send_sem=ag_s, recv_sem=ag_r,
-            **device(i)).start()
-
+    def hail(p, s):
+        pl.semaphore_signal(barrier, inc=1, **device(p, s))
+
+    host, guest = device(mp - 1, ms), device(mp + 1, ms)
     visit = [
         pltpu.make_async_remote_copy(
-            src_ref=src, dst_ref=dst, send_sem=mate_s.at[i], recv_sem=mate_r.at[i],
-            **device(me - shift))
-        for i, (src, dst) in enumerate(((cs_h, mate_cs), (cr_h, mate_cr), (ced_h, mate_v)))
-    ]
+            src_ref=src, dst_ref=dst, send_sem=out, recv_sem=sem, **host)
+        for src, dst, out, sem in (
+            (ced_h, mate_v, sent, mate_r),
+            (cs_h, mate_ids.at[0], ids_r, ids_r), (cr_h, mate_ids.at[1], ids_r, ids_r))
+    ]
+    await_ids = pltpu.make_async_copy(mate_ids, mate_ids, ids_r).wait
     back = pltpu.make_async_remote_copy(
-        src_ref=mate_new, dst_ref=mate_v, send_sem=back_s, recv_sem=back_r, **device(me + shift))
-
-    def away(i):
-        return jnp.where(i >= hubs, 1, 0)
-
-    prev, after = turn(me, group - 1, group), turn(me, 1, group)
-    callers = away(prev) + away(after) + jnp.where(
-        hosts, 1 + away(me + shift - 1) + away(turn(me + shift, 1, group)), 0)
+        src_ref=mate_new, dst_ref=mate_v, send_sem=sent, recv_sem=mate_r, **guest)
+
+    @pl.when(hub)
+    def _():
+        pl.when(hosts)(lambda: hail(mp + 1, ms))
+        each(hub_p - 1, lambda i: patch(turn(mp, i + 1, hub_p), hail))
+        beside(hail)
 
     @pl.when(leaf)
     def _():
-        pl.semaphore_wait(barrier, hubs)
-        each(hubs, lambda i: send_head(hubs - 1 - i))
+        pl.semaphore_wait(barrier, 1)
         for copy in visit:
             copy.start()
-        pl.semaphore_signal(near, inc=1, **device(me - shift))
-        for beside in (prev, after):
-            pl.semaphore_signal(near, inc=1, **device(beside - shift * away(beside)))
-
-    pairs = [
-        (nodes_h, nodes_v), (hl_h, hl_v), (fs_h, fs_v), (fr_h, fr_v), (cs_h, cs_v), (cr_h, cr_v),
-        (wei_h, wei_v), (edges_h, edges_v), (ced_h, ced_v),
-        (weo_h, weo_v), (wni_h, wni_v), (wno_h, wno_v),
-    ]
-    loads = [pltpu.make_async_copy(h, v, in_sem.at[i]) for i, (h, v) in enumerate(pairs)]
-    for copy in loads:
-        copy.start()
-    (l_nodes, l_hl, l_fs, l_fr, l_cs, l_cr, l_wei, l_edges, l_ced, l_weo, l_wni, l_wno) = loads
-
-    l_nodes.wait()
+
+    groups = [
+        [(nodes_h, nodes_v), (hl_h, hl_v)],
+        [(fs_h, fs_v), (fr_h, fr_v), (cs_h, cs_v), (cr_h, cr_v), (wei_h, wei_v)],
+        [(edges_h, edges_v), (ced_h, ced_v), (weo_h, weo_v), (wni_h, wni_v), (wno_h, wno_v)],
+    ]
+    loads = [[pltpu.make_async_copy(h, v, in_sem.at[i]) for h, v in pairs]
+             for i, pairs in enumerate(groups)]
+    for copies in loads:
+        for copy in copies:
+            copy.start()
+
+    def loaded(i):
+        for copy in loads[i]:
+            copy.wait()
+
+    loaded(0)
     nodes = nodes_v[...]
-    l_hl.wait()
+    head_row = heads_r.at[me]
+
+    def send_head(p, s):
+        pltpu.make_async_remote_copy(
+            src_ref=head_row, dst_ref=head_row, send_sem=ag_s, recv_sem=ag_r,
+            **device(p, s)).start()
+
+    heads_r[me] = nodes[:co]
+
+    @pl.when(hub)
+    def _():
+        pl.semaphore_wait(barrier, hubs - 1)
+        pl.when(hosts)(lambda: hail(mp + 1, ms))
+        each(hub_p - 1, lambda i: patch(turn(mp, hub_p - 1 - i, hub_p), send_head))
+        beside(send_head)
+
     for side in range(2):
         pick = hot_t(hl_v[0, side:side + 1, :], nodes_n)
         halo_s[side] = dot(pick, nodes, ((0,), (0,))).astype(BF16)
 
-    @pl.when(hub)
-    def _():
-        heads_r[me] = nodes_v[:co]
-        pl.semaphore_wait(barrier, hubs - 1)
-        each(hubs, lambda i: pl.when(hubs - 1 - i != me)(lambda: send_head(hubs - 1 - i)))
+    prev, after = turn(me, group - 1, group), turn(me, 1, group)
+
+    def away(i):
+        return jnp.where(i >= hubs, 1, 0)
+
+    @pl.when(leaf)
+    def _():
+        pl.semaphore_wait(barrier, 1)
+        each(hub_p, lambda i: patch(hub_p - 1 - i, send_head))
+        pl.semaphore_signal(near, inc=1, **host)
+        for i in (prev, after):
+            pl.semaphore_signal(near, inc=1, **device_of(i - shift * away(i)))
 
     halos, soon = [], []
     for side, to in ((0, after), (1, prev)):
         soon.append(to < hubs)
         halos.append(pltpu.make_async_remote_copy(
             src_ref=halo_s.at[side], dst_ref=halo_r.at[side],
-            send_sem=halo_ss.at[side], recv_sem=halo_rs.at[side], **device(to)))
+            send_sem=sent, recv_sem=halo_rs, **device_of(to)))
         pl.when(soon[-1])(halos[-1].start)
 
-    l_fs.wait()
-    l_fr.wait()
-    l_cs.wait()
-    l_cr.wait()
+    loaded(1)
     fs, fr = fs_v[...], fr_v[...]
     fs_col = column(jnp.where(fs < halo, fs + (nodes_n + halo), fs - halo))
     fr_col = column(fr)
-
-    l_wei.wait()
     own = jnp.concatenate(
         [dot(nodes, wei_v[d:2 * d]).astype(BF16), dot(nodes, wei_v[2 * d:]).astype(BF16)], axis=0)
     sel = jnp.concatenate([hot(fs_col, 0, nodes_n), hot(fr_col, 0, nodes_n)], axis=1)
-    l_edges.wait()
-    l_ced.wait()
+    loaded(2)
     acc[...] = dot(edges_v[...], wei_v[:d]) + dot(sel, own)
-    l_weo.wait()
-    l_wni.wait()
-    l_wno.wait()
-
+
+    callers = away(prev) + away(after) + jnp.where(
+        hosts, 1 + away(me + shift - 1) + away(turn(me + shift, 1, group)), 0)
     pl.when(hub & (callers > 0))(lambda: pl.semaphore_wait(near, callers))
-    pl.when(hosts)(lambda: pl.semaphore_signal(go, inc=1, **device(me + shift)))
-    pl.when(leaf)(lambda: pl.semaphore_wait(go, 1))
+    pl.when(hosts)(lambda: pl.semaphore_signal(near, inc=1, **guest))
+    pl.when(leaf)(lambda: pl.semaphore_wait(near, 1))
     for early, copy in zip(soon, halos):
         pl.when(jnp.logical_not(early))(copy.start)
 
@@ -203,16 +220,15 @@
         ced, cs, cr = ced_v[...], cs_v[...], cr_v[...]
         ced_pre = dot(ced, wei_v[:d])
         if hosting:
-            visit[0].wait_recv()
-            visit[1].wait_recv()
-            cs = jnp.concatenate([cs, mate_cs[...]], axis=1)
-            cr = jnp.concatenate([cr, mate_cr[...]], axis=1)
+            await_ids()
+            cs = jnp.concatenate([cs, mate_ids[0]], axis=1)
+            cr = jnp.concatenate([cr, mate_ids[1]], axis=1)
         rows = cs.shape[1]
         picks = hot_t(cr, group * co)
         ends = jnp.concatenate(
             [hot(column(cs), 0, group * co), hot(column(cr), 0, group * co)], axis=0)
         if hosting:
-            visit[2].wait_recv()
+            visit[0].wait_recv()
             ced_pre = jnp.concatenate([ced_pre, dot(mate_v[...], wei_v[:d])], axis=0)
             ced = jnp.concatenate([ced, mate_v[...]], axis=0)
 
@@ -234,7 +250,7 @@
         def send_part(i):
             pltpu.make_async_remote_copy(
                 src_ref=part_s.at[i], dst_ref=part_r.at[me],
-                send_sem=rs_s, recv_sem=rs_r, **device(i)).start()
+                send_sem=rs_s, recv_sem=rs_r, **device_of(i)).start()
 
         def pack(i):
             both = part_f[rows_of(i), :].astype(BF16)
@@ -253,8 +269,7 @@
     pl.when(hub & jnp.logical_not(hosts))(lambda: coarse(False))
     pl.when(hosts)(lambda: coarse(True))
 
-    for copy in halos:
-        copy.wait_recv()
+    pltpu.make_async_copy(halo_r, halo_r, halo_rs).wait()
     far = dot(jnp.concatenate([halo_r[1], halo_r[0]], axis=0), wei_v[d:2 * d]).astype(BF16)
     hid = silu(acc[...] + dot(hot(fs_col, nodes_n, 2 * halo), far))
     delta = norm_rows(dot(hid, weo_v[...]))
@@ -268,10 +283,12 @@
     n_pre[...] = pre[:first]
     top[...] = fine[:first]
 
-    for copy in halos:
-        copy.wait_send()
-
-    pl.when(hosts)(back.wait_send)
+    def await_sent(rows):
+        span = edges_v.at[pl.ds(0, rows)]
+        pltpu.make_async_copy(span, span, sent).wait()
+
+    pl.when(mp < hub_p - 1)(lambda: await_sent(2 * halo))
+    pl.when(mp >= hub_p - 1)(lambda: await_sent(2 * halo + count))
 
     @pl.when(hub)
     def _():
@@ -282,8 +299,7 @@
     @pl.when(leaf)
     def _():
         await_rows(hubs, ag_s)
-        for copy in visit:
-            copy.wait_send()
+        await_ids()
         back.wait_recv()
         nc_v[...] = mate_v[...]
         await_rows(hubs, rs_r)
@@ -334,8 +350,7 @@
     scratch = [pltpu.VMEM(x.shape, x.dtype) for x in (edges, ced, wei, weo, fs, fr, hl, cs, cr)] + [
         pltpu.VMEM((c, d), BF16),
         pltpu.VMEM((c, d), BF16),
-        pltpu.VMEM(cs.shape, cs.dtype),
-        pltpu.VMEM(cr.shape, cr.dtype),
+        pltpu.VMEM((2,) + cs.shape, cs.dtype),
         pltpu.VMEM((group, CO_DEV, d), BF16),
         pltpu.VMEM((group * CO_DEV, d), F32),
         pltpu.VMEM((2, halo, d), BF16),
@@ -344,8 +359,7 @@
         pltpu.VMEM((group, CO_DEV, d), BF16),
         pltpu.VMEM((group - n_sub, CO_DEV, d), BF16),
         pltpu.VMEM((e, d), F32),
-        dma((12,)), dma, dma, dma((2,)), dma((2,)), dma, dma, dma((3,)), dma((3,)), dma, dma,
-        pltpu.SemaphoreType.REGULAR, pltpu.SemaphoreType.REGULAR,
+        dma((3,)), dma, dma, dma, dma, dma, dma, dma, dma, pltpu.SemaphoreType.REGULAR,
     ]
     held = pl.pallas_call(
         functools.partial(kernel, n_patch, n_sub),

time: 15.9 us -> 15.3 us (0.962)
  Pallas kernels: 15.1 us -> 14.5 us
    pallas_call x1, Pallas kernels: 14 us -> 13.3 us  [body(): pl.pallas_call(functools.partial(kernel, n_patch, n_sub), out_shape=kept,...]
where the time goes in v3:
time: 15.3 us; the launch traced here: 15.1 us
  Pallas kernels  14.5 us (95%)
  between operations  0.64 us (4%)
    pallas_call x1, Pallas kernels, body(): pl.pallas_call(functools.partial(kernel, n_patch, n_sub), out_shape=kept,...  13.3 us
    pallas_call x1, Pallas kernels, body(): pl.pallas_call(finish, out_shape=[jax.ShapeDtypeStruct(x.shape, BF16) for...  1.16 us

profile of v3, /device:TPU:0, one launch (start us, length us, event | category | flops | bytes accessed | tf_op | source)
XLA Modules:
  0.0 15.1 jit_solution(3851614353481687708)
XLA Ops:
  0.6 13.3 %layer.1 = (bf16[128,512]{1,0:T(8,128)(2,1)S(1)}, bf16[512,512]{1,0:T(8,128)(2,1)S(1)}, bf16[64,512]{1,0:T(8,128)(2,1)S(1)}, bf16[128,512]{1,0:T(8,128)(2,1)S(1)...) custom-call(bf16[128,512]{1,0:T(8,128)(2,1)} %nodes_h.1, ...), custom_call_target="tpu_custom_call" | custom-call | tf_op jit(solution)/shard_map/layer/pallas_call | solution.py:364
  14.0 1.2 %finish.1 = (bf16[128,512]{1,0:T(8,128)(2,1)}, bf16[512,512]{1,0:T(8,128)(2,1)}, bf16[64,512]{1,0:T(8,128)(2,1)}) custom-call(bf16[128,512]{1,0:T(8,128)(2,1)S(1)} %get-tuple-element.11.n_rows, bf16[512,512]{1,0:T(8,128)(2,1)S(1)} %get-tuple-element.12.ne_v, bf16[64,512]{1,0:T(8,128)(2,1)S(1)} %get-tuple-element.13.nc_v, ...), custom_call_target="tpu_custom_call" | custom-call | tf_op jit(solution)/shard_map/finish/pallas_call | solution.py:374

commit v4 on v3

--- a/solution.py
+++ b/solution.py
@@ -68,7 +68,7 @@
     edges_v, ced_v, wei_v, weo_v, fs_v, fr_v, hl_v, cs_v, cr_v,
     mate_v, mate_new, mate_ids,
     heads_r, heads_f, halo_s, halo_r, part_f, part_s, part_r,
-    acc, in_sem, sent, ag_s, ag_r, halo_rs, rs_s, rs_r, ids_r, mate_r, near,
+    acc, ced_pre, in_sem, sent, ag_s, ag_r, halo_rs, rs_s, rs_r, ids_r, mate_r, near,
 ):
     group, shift = n_patch * n_sub, n_sub
     hub_p = n_patch - 1
@@ -97,14 +97,14 @@
             return device(i // n_sub, i % n_sub)
         return device(lax.div(i, n_sub), lax.rem(i, n_sub))
 
-    subs = [ms] + [turn(ms, j, n_sub) for j in range(1, n_sub)]
+    subs = [turn(ms, j, n_sub) for j in list(range(n_sub // 2, n_sub)) + list(range(1, n_sub // 2))]
 
     def patch(p, step):
+        for s in subs + [ms]:
+            step(p, s)
+
+    def beside(step):
         for s in subs:
-            step(p, s)
-
-    def beside(step):
-        for s in subs[1:]:
             step(mp, s)
 
     def await_rows(number, sem):
@@ -130,8 +130,9 @@
 
     @pl.when(hub)
     def _():
+        patch(turn(mp, 1, hub_p), hail)
         pl.when(hosts)(lambda: hail(mp + 1, ms))
-        each(hub_p - 1, lambda i: patch(turn(mp, i + 1, hub_p), hail))
+        each(hub_p - 2, lambda i: patch(turn(mp, i + 2, hub_p), hail))
         beside(hail)
 
     @pl.when(leaf)
@@ -173,10 +174,6 @@
         each(hub_p - 1, lambda i: patch(turn(mp, hub_p - 1 - i, hub_p), send_head))
         beside(send_head)
 
-    for side in range(2):
-        pick = hot_t(hl_v[0, side:side + 1, :], nodes_n)
-        halo_s[side] = dot(pick, nodes, ((0,), (0,))).astype(BF16)
-
     prev, after = turn(me, group - 1, group), turn(me, 1, group)
 
     def away(i):
@@ -189,6 +186,10 @@
         pl.semaphore_signal(near, inc=1, **host)
         for i in (prev, after):
             pl.semaphore_signal(near, inc=1, **device_of(i - shift * away(i)))
+
+    for side in range(2):
+        pick = hot_t(hl_v[0, side:side + 1, :], nodes_n)
+        halo_s[side] = dot(pick, nodes, ((0,), (0,))).astype(BF16)
 
     halos, soon = [], []
     for side, to in ((0, after), (1, prev)):
@@ -218,7 +219,7 @@
 
     def coarse(hosting):
         ced, cs, cr = ced_v[...], cs_v[...], cr_v[...]
-        ced_pre = dot(ced, wei_v[:d])
+        ced_pre[:count] = dot(ced, wei_v[:d])
         if hosting:
             await_ids()
             cs = jnp.concatenate([cs, mate_ids[0]], axis=1)
@@ -229,7 +230,7 @@
             [hot(column(cs), 0, group * co), hot(column(cr), 0, group * co)], axis=0)
         if hosting:
             visit[0].wait_recv()
-            ced_pre = jnp.concatenate([ced_pre, dot(mate_v[...], wei_v[:d])], axis=0)
+            ced_pre[count:] = dot(mate_v[...], wei_v[:d])
             ced = jnp.concatenate([ced, mate_v[...]], axis=0)
 
         await_rows(group - 1, ag_r)
@@ -243,7 +244,7 @@
         heads = heads_f[...].astype(BF16)
         c_ends = dot(ends, heads).astype(BF16)
         c_in = jnp.concatenate([c_ends[:rows], c_ends[rows:]], axis=1)
-        c_hid = silu(ced_pre + dot(c_in, wei_v[d:]))
+        c_hid = silu(ced_pre[:rows] + dot(c_in, wei_v[d:]))
         c_new = (ced.astype(F32) + norm_rows(dot(c_hid, weo_v[...]))).astype(BF16)
         part_f[...] = dot(picks, c_new)
 
@@ -310,20 +311,15 @@
 def finish(n_rows, ne_v, nc_v, nodes_v, n_pre, top, wni_v, wno_v, nn_h, ne_h, nc_h, first_v, sem):
     first, d = top.shape
     n = n_rows.shape[0]
-    copies = [
-        pltpu.make_async_copy(ne_v, ne_h, sem.at[0]),
-        pltpu.make_async_copy(nc_v, nc_h, sem.at[1]),
-        pltpu.make_async_copy(n_rows.at[pl.ds(first, n - first)], nn_h.at[pl.ds(first, n - first)],
-                              sem.at[2]),
-    ]
-    for copy in copies:
-        copy.start()
+    for src, dst in (
+            (ne_v, ne_h), (nc_v, nc_h),
+            (n_rows.at[pl.ds(first, n - first)], nn_h.at[pl.ds(first, n - first)])):
+        pltpu.make_async_copy(src, dst, sem).start()
     pre = n_pre[...] + dot(top[...].astype(BF16), wni_v[d:])
     first_v[...] = node_rows(nodes_v[:first], pre, wno_v[...])
-    copies.append(pltpu.make_async_copy(first_v, nn_h.at[pl.ds(0, first)], sem.at[3]))
-    copies[-1].start()
-    for copy in copies:
-        copy.wait()
+    pltpu.make_async_copy(first_v, nn_h.at[pl.ds(0, first)], sem).start()
+    span = wni_v.at[pl.ds(0, ne_v.shape[0] + nc_v.shape[0] + n)]
+    pltpu.make_async_copy(span, span, sem).wait()
 
 
 def body(n_patch, n_sub, *args):
@@ -359,6 +355,7 @@
         pltpu.VMEM((group, CO_DEV, d), BF16),
         pltpu.VMEM((group - n_sub, CO_DEV, d), BF16),
         pltpu.VMEM((e, d), F32),
+        pltpu.VMEM((2 * c, d), F32),
         dma((3,)), dma, dma, dma, dma, dma, dma, dma, dma, pltpu.SemaphoreType.REGULAR,
     ]
     held = pl.pallas_call(
@@ -376,7 +373,7 @@
         out_shape=[jax.ShapeDtypeStruct(x.shape, BF16) for x in (nodes, edges, ced)],
         in_specs=[inside] * len(kept),
         out_specs=[anywhere] * 3,
-        scratch_shapes=[pltpu.VMEM((FIRST, d), BF16), dma((4,))],
+        scratch_shapes=[pltpu.VMEM((FIRST, d), BF16), dma],
         compiler_params=pltpu.CompilerParams(vmem_limit_bytes=8 * 1024 * 1024),
         name="finish",
     )(*held)

time: 15.3 us -> 15.1 us (0.987)
  Pallas kernels: 14.5 us -> 14.3 us
where the time goes in v4:
time: 15.1 us; the launch traced here: 15 us
  Pallas kernels  14.3 us (95%)
  between operations  0.64 us (4%)
    pallas_call x1, Pallas kernels, body(): pl.pallas_call(functools.partial(kernel, n_patch, n_sub), out_shape=kept,...  13.2 us
    pallas_call x1, Pallas kernels, body(): pl.pallas_call(finish, out_shape=[jax.ShapeDtypeStruct(x.shape, BF16) for...  1.13 us

profile of v4, /device:TPU:0, one launch (start us, length us, event | category | flops | bytes accessed | tf_op | source)
XLA Modules:
  0.0 15.0 jit_solution(13895889707565958239)
XLA Ops:
  0.6 13.2 %layer.1 = (bf16[128,512]{1,0:T(8,128)(2,1)S(1)}, bf16[512,512]{1,0:T(8,128)(2,1)S(1)}, bf16[64,512]{1,0:T(8,128)(2,1)S(1)}, bf16[128,512]{1,0:T(8,128)(2,1)S(1)...) custom-call(bf16[128,512]{1,0:T(8,128)(2,1)} %nodes_h.1, ...), custom_call_target="tpu_custom_call" | custom-call | tf_op jit(solution)/shard_map/layer/pallas_call | solution.py:361
  13.8 1.1 %finish.1 = (bf16[128,512]{1,0:T(8,128)(2,1)}, bf16[512,512]{1,0:T(8,128)(2,1)}, bf16[64,512]{1,0:T(8,128)(2,1)}) custom-call(bf16[128,512]{1,0:T(8,128)(2,1)S(1)} %get-tuple-element.11.n_rows, bf16[512,512]{1,0:T(8,128)(2,1)S(1)} %get-tuple-element.12.ne_v, bf16[64,512]{1,0:T(8,128)(2,1)S(1)} %get-tuple-element.13.nc_v, ...), custom_call_target="tpu_custom_call" | custom-call | tf_op jit(solution)/shard_map/finish/pallas_call | solution.py:371

commit v5 on v4

--- a/solution.py
+++ b/solution.py
@@ -23,9 +23,14 @@
     return (half + half * jnp.tanh(half)).astype(BF16)
 
 
-def norm_rows(values):
-    mean = jnp.mean(values, axis=-1, keepdims=True)
-    centred = values - mean
+def centre(w):
+    n = w.shape[1]
+    mean = dot(w, jnp.full((n, 128), 1.0, BF16)) * (1.0 / n)
+    return jnp.concatenate(
+        [(w[:, i:i + 128].astype(F32) - mean).astype(BF16) for i in range(0, n, 128)], axis=1)
+
+
+def norm_rows(centred):
     return centred * lax.rsqrt(jnp.mean(centred * centred, axis=-1, keepdims=True) + 1e-05)
 
 
@@ -68,7 +73,7 @@
     edges_v, ced_v, wei_v, weo_v, fs_v, fr_v, hl_v, cs_v, cr_v,
     mate_v, mate_new, mate_ids,
     heads_r, heads_f, halo_s, halo_r, part_f, part_s, part_r,
-    acc, ced_pre, in_sem, sent, ag_s, ag_r, halo_rs, rs_s, rs_r, ids_r, mate_r, near,
+    acc, ced_pre, weo_raw, wno_raw, in_sem, sent, ag_s, ag_r, halo_rs, rs_s, rs_r, ids_r, mate_r, near,
 ):
     group, shift = n_patch * n_sub, n_sub
     hub_p = n_patch - 1
@@ -144,7 +149,7 @@
     groups = [
         [(nodes_h, nodes_v), (hl_h, hl_v)],
         [(fs_h, fs_v), (fr_h, fr_v), (cs_h, cs_v), (cr_h, cr_v), (wei_h, wei_v)],
-        [(edges_h, edges_v), (ced_h, ced_v), (weo_h, weo_v), (wni_h, wni_v), (wno_h, wno_v)],
+        [(edges_h, edges_v), (ced_h, ced_v), (weo_h, weo_raw), (wni_h, wni_v), (wno_h, wno_raw)],
     ]
     loads = [[pltpu.make_async_copy(h, v, in_sem.at[i]) for h, v in pairs]
              for i, pairs in enumerate(groups)]
@@ -170,7 +175,12 @@
     @pl.when(hub)
     def _():
         pl.semaphore_wait(barrier, hubs - 1)
-        pl.when(hosts)(lambda: hail(mp + 1, ms))
+
+        @pl.when(hosts & (lax.rem(ms, 2) == 0))
+        def _():
+            hail(mp + 1, ms)
+            hail(mp + 1, ms + 1)
+
         each(hub_p - 1, lambda i: patch(turn(mp, hub_p - 1 - i, hub_p), send_head))
         beside(send_head)
 
@@ -208,6 +218,8 @@
     sel = jnp.concatenate([hot(fs_col, 0, nodes_n), hot(fr_col, 0, nodes_n)], axis=1)
     loaded(2)
     acc[...] = dot(edges_v[...], wei_v[:d]) + dot(sel, own)
+    weo_v[...] = centre(weo_raw[...])
+    wno_v[...] = centre(wno_raw[...])
 
     callers = away(prev) + away(after) + jnp.where(
         hosts, 1 + away(me + shift - 1) + away(turn(me + shift, 1, group)), 0)
@@ -356,6 +368,8 @@
         pltpu.VMEM((group - n_sub, CO_DEV, d), BF16),
         pltpu.VMEM((e, d), F32),
         pltpu.VMEM((2 * c, d), F32),
+        pltpu.VMEM(weo.shape, BF16),
+        pltpu.VMEM(wno.shape, BF16),
         dma((3,)), dma, dma, dma, dma, dma, dma, dma, dma, pltpu.SemaphoreType.REGULAR,
     ]
     held = pl.pallas_call(

time: 15.1 us -> 15.2 us (level)
  no operation moved by 1% of the time
where the time goes in v5:
time: 15.2 us; the launch traced here: 15 us
  Pallas kernels  14.4 us (95%)
  between operations  0.64 us (4%)
    pallas_call x1, Pallas kernels, body(): pl.pallas_call(functools.partial(kernel, n_patch, n_sub), out_shape=kept,...  13.3 us
    pallas_call x1, Pallas kernels, body(): pl.pallas_call(finish, out_shape=[jax.ShapeDtypeStruct(x.shape, BF16) for...  1.05 us

profile of v5, /device:TPU:0, one launch (start us, length us, event | category | flops | bytes accessed | tf_op | source)
XLA Modules:
  0.0 15.0 jit_solution(2714506073505007897)
XLA Ops:
  0.6 13.3 %layer.1 = (bf16[128,512]{1,0:T(8,128)(2,1)S(1)}, bf16[512,512]{1,0:T(8,128)(2,1)S(1)}, bf16[64,512]{1,0:T(8,128)(2,1)S(1)}, bf16[128,512]{1,0:T(8,128)(2,1)S(1)...) custom-call(bf16[128,512]{1,0:T(8,128)(2,1)} %nodes_h.1, ...), custom_call_target="tpu_custom_call" | custom-call | tf_op jit(solution)/shard_map/layer/pallas_call | solution.py:375
  14.0 1.1 %finish.1 = (bf16[128,512]{1,0:T(8,128)(2,1)}, bf16[512,512]{1,0:T(8,128)(2,1)}, bf16[64,512]{1,0:T(8,128)(2,1)}) custom-call(bf16[128,512]{1,0:T(8,128)(2,1)S(1)} %get-tuple-element.11.n_rows, bf16[512,512]{1,0:T(8,128)(2,1)S(1)} %get-tuple-element.12.ne_v, bf16[64,512]{1,0:T(8,128)(2,1)S(1)} %get-tuple-element.13.nc_v, ...), custom_call_target="tpu_custom_call" | custom-call | tf_op jit(solution)/shard_map/finish/pallas_call | solution.py:385

commit v6 on v5

--- a/solution.py
+++ b/solution.py
@@ -175,12 +175,7 @@
     @pl.when(hub)
     def _():
         pl.semaphore_wait(barrier, hubs - 1)
-
-        @pl.when(hosts & (lax.rem(ms, 2) == 0))
-        def _():
-            hail(mp + 1, ms)
-            hail(mp + 1, ms + 1)
-
+        pl.when(hosts)(lambda: hail(mp + 1, ms))
         each(hub_p - 1, lambda i: patch(turn(mp, hub_p - 1 - i, hub_p), send_head))
         beside(send_head)
 

time: 15.2 us -> 15 us (0.987)
  Pallas kernels: 14.4 us -> 14.2 us
    pallas_call x1, Pallas kernels: 13.3 us -> 13.1 us  [body(): pl.pallas_call(functools.partial(kernel, n_patch, n_sub), out_shape=kept,...]
where the time goes in v6:
time: 15 us; the launch traced here: 14.8 us
  Pallas kernels  14.2 us (95%)
  between operations  0.64 us (4%)
    pallas_call x1, Pallas kernels, body(): pl.pallas_call(functools.partial(kernel, n_patch, n_sub), out_shape=kept,...  13.1 us
    pallas_call x1, Pallas kernels, body(): pl.pallas_call(finish, out_shape=[jax.ShapeDtypeStruct(x.shape, BF16) for...  1.05 us

profile of v6, /device:TPU:0, one launch (start us, length us, event | category | flops | bytes accessed | tf_op | source)
XLA Modules:
  0.0 14.8 jit_solution(15208160310717498894)
XLA Ops:
  0.6 13.1 %layer.1 = (bf16[128,512]{1,0:T(8,128)(2,1)S(1)}, bf16[512,512]{1,0:T(8,128)(2,1)S(1)}, bf16[64,512]{1,0:T(8,128)(2,1)S(1)}, bf16[128,512]{1,0:T(8,128)(2,1)S(1)...) custom-call(bf16[128,512]{1,0:T(8,128)(2,1)} %nodes_h.1, ...), custom_call_target="tpu_custom_call" | custom-call | tf_op jit(solution)/shard_map/layer/pallas_call | solution.py:370
  13.8 1.1 %finish.1 = (bf16[128,512]{1,0:T(8,128)(2,1)}, bf16[512,512]{1,0:T(8,128)(2,1)}, bf16[64,512]{1,0:T(8,128)(2,1)}) custom-call(bf16[128,512]{1,0:T(8,128)(2,1)S(1)} %get-tuple-element.11.n_rows, bf16[512,512]{1,0:T(8,128)(2,1)S(1)} %get-tuple-element.12.ne_v, bf16[64,512]{1,0:T(8,128)(2,1)S(1)} %get-tuple-element.13.nc_v, ...), custom_call_target="tpu_custom_call" | custom-call | tf_op jit(solution)/shard_map/finish/pallas_call | solution.py:380
